TPU v7x, 32 devices: a whole 2x2x4 slice. The times are simulated.
32 devices in a mesh: shard: 4 (over y, x), replica: 8 (over z, core).
Axes of the slice: x: 2, y: 2, z: 4, core: 2. Of those that a mesh axis runs over, the one named last changes fastest.
Arguments:
- tokens: bfloat16 [8192, 1536], P(('shard', 'replica')), may hold values from -6 to 6
- cotangent: bfloat16 [8192, 1536], P(('shard', 'replica')), may hold values from -6 to 6
- seq_lengths: int32 [64], replicated, may hold values from 0 to 256, as said below
- seq_device: int32 [64], replicated, may hold values from 0 to 31
- seq_offsets: int32 [64], replicated, may hold values from 0 to 1
- norm_attn: bfloat16 [1, 1536], P(None, 'shard'), may hold values from 0.5 to 1.5
- w_qkv: bfloat16 [1, 1536, 3072], P(None, 'shard'), may hold values from -0.15625 to 0.15625
- w_out: bfloat16 [1, 1536, 1536], P(None, 'shard'), may hold values from -0.625 to 0.625
- norm_mlp: bfloat16 [1, 1536], P(None, 'shard'), may hold values from 0.5 to 1.5
- w_gate_up: bfloat16 [1, 1536, 8192], P(None, 'shard'), may hold values from -0.15625 to 0.15625
- w_down: bfloat16 [1, 4096, 1536], P(None, 'shard'), may hold values from -0.125 to 0.125
Outputs:
- result: bfloat16 [8192, 1536], P(('shard', 'replica'))
- grad_tokens: float32 [8192, 1536], P(('shard', 'replica'))
- grad_norm_attn: float32 [1, 1536], P(None, 'shard')
- grad_w_qkv: float32 [1, 1536, 3072], P(None, 'shard')
- grad_w_out: float32 [1, 1536, 1536], P(None, 'shard')
- grad_norm_mlp: float32 [1, 1536], P(None, 'shard')
- grad_w_gate_up: float32 [1, 1536, 8192], P(None, 'shard')
- grad_w_down: float32 [1, 4096, 1536], P(None, 'shard')
Inputs may be any that keep to these rules, and one draw needn't show every extreme that they name: `seq_lengths`: each device is named by exactly 2 entries. A sequence lies within blocks 2p and 2p + 1 of its device for some p; sequences of one device never share a row; length 0 marks an unused entry. In every draw some device is full, its every pair of blocks holding one sequence of length 256.
All inputs are finite; a program needn't handle non-finite values.
Results may differ from a plain program's by a relative error of at most 0.02.
Values may be sent and summed in bfloat16 or wider, within the bound.
A program may use at most 320 MiB of HBM per device.

v0:
```python
import jax
import jax.numpy as jnp
from jax import lax
from jax.sharding import PartitionSpec as P

HEADS = 16
KV_HEADS = 8
HEAD = 96
FF = 4096
BLOCK = 128
epsilon = 1e-05
rope_base = 100000.0


def rms_scale(field):
    return lax.rsqrt(jnp.mean(field * field, axis=-1, keepdims=True) + epsilon)


def rotate(field):
    half = field.shape[-1] // 2
    return jnp.concatenate([-field[..., half:], field[..., :half]], axis=-1)


def rope_tables(position):
    half = HEAD // 2
    freqs = rope_base ** (-(jnp.arange(half, dtype=jnp.float32) * 2.0) / HEAD)
    angles = position.astype(jnp.float32)[:, None] * freqs[None, :]
    cosine = jnp.cos(angles)
    sine = jnp.sin(angles)
    return (jnp.concatenate([cosine, cosine], axis=-1), jnp.concatenate([sine, sine], axis=-1))


def locate(device, seq_lengths, seq_device, seq_offsets, rows):
    starts = seq_offsets * BLOCK
    local = jnp.arange(rows, dtype=jnp.int32)
    labels = jnp.arange(seq_lengths.shape[0], dtype=jnp.int32)
    hits = (
        (seq_device[None, :] == device)
        & (local[:, None] >= starts[None, :])
        & (local[:, None] < (starts + seq_lengths)[None, :])
    )
    segment = jnp.max(jnp.where(hits, labels[None, :], -1), axis=1)
    begin = jnp.sum(jnp.where(hits, starts[None, :], 0), axis=1)
    return (segment, local - begin)


def mask_of(segment):
    local = jnp.arange(segment.shape[0], dtype=jnp.int32)
    return (segment[:, None] == segment[None, :]) & (local[None, :] <= local[:, None])


def contract_rows(left, right):
    return lax.dot_general(
        left, right, (((0,), (0,)), ((), ())), preferred_element_type=jnp.float32
    )


def contract_cols(left, right):
    return lax.dot_general(
        left, right, (((1,), (1,)), ((), ())), preferred_element_type=jnp.float32
    )


def norm_rows(field, gain):
    scale = rms_scale(field)
    normed = (field * scale * gain.astype(jnp.float32)[None, :]).astype(jnp.bfloat16)
    return (scale, normed)


def norm_back(grad_normed, field, scale, gain):
    normed = field * scale
    grad_gain = jnp.sum(grad_normed * normed, axis=0)
    inner = grad_normed * gain[None, :]
    grad_field = scale * (inner - normed * jnp.mean(inner * normed, axis=-1, keepdims=True))
    return (grad_field, grad_gain)


def split_project(project, q_heads, k_heads, cosine, sine):
    rows = project.shape[0]
    width_q = q_heads * HEAD
    width_k = k_heads * HEAD
    queries = project[:, :width_q].reshape(rows, q_heads, HEAD)
    keys = project[:, width_q : width_q + width_k].reshape(rows, k_heads, HEAD)
    values_b = project[:, width_q + width_k :].reshape(rows, k_heads, HEAD).astype(jnp.bfloat16)
    queries_b = (queries * cosine[:, None, :] + rotate(queries) * sine[:, None, :]).astype(
        jnp.bfloat16
    )
    keys_b = (keys * cosine[:, None, :] + rotate(keys) * sine[:, None, :]).astype(jnp.bfloat16)
    return (queries_b, keys_b, values_b)


def join_grads(grad_queries, grad_keys, grad_values, cosine, sine):
    rows = grad_queries.shape[0]
    grad_queries = grad_queries * cosine[:, None, :] - rotate(grad_queries * sine[:, None, :])
    grad_keys = grad_keys * cosine[:, None, :] - rotate(grad_keys * sine[:, None, :])
    return jnp.concatenate(
        [
            grad_queries.reshape(rows, -1),
            grad_keys.reshape(rows, -1),
            grad_values.reshape(rows, -1),
        ],
        axis=1,
    ).astype(jnp.bfloat16)


def attention_scores(queries_b, keys_b, allowed):
    rows = queries_b.shape[0]
    kv_count = keys_b.shape[1]
    grouped = queries_b.reshape(rows, kv_count, queries_b.shape[1] // kv_count, HEAD)
    scores = jnp.einsum(
        "qkgd,pkd->kgqp", grouped, keys_b, preferred_element_type=jnp.float32
    ) * HEAD ** (-0.5)
    return jnp.where(allowed, scores, -1e30)


def attend_forward(queries_b, keys_b, values_b, allowed):
    rows = queries_b.shape[0]
    scores = attention_scores(queries_b, keys_b, allowed)
    top = jnp.max(scores, axis=-1, keepdims=True)
    total = jnp.log(jnp.sum(jnp.exp(scores - top), axis=-1, keepdims=True)) + top
    weights_b = jnp.exp(scores - total).astype(jnp.bfloat16)
    mixed = jnp.einsum("kgqp,pkd->qkgd", weights_b, values_b, preferred_element_type=jnp.float32)
    return (mixed.reshape(rows, -1).astype(jnp.bfloat16), total)


def attend_backward(grad_mixed_b, queries_b, keys_b, values_b, total, allowed):
    rows = queries_b.shape[0]
    q_heads = queries_b.shape[1]
    kv_count = keys_b.shape[1]
    per = q_heads // kv_count
    factor = HEAD ** (-0.5)
    grad_mixed = grad_mixed_b.reshape(rows, kv_count, per, HEAD)
    weights = jnp.exp(attention_scores(queries_b, keys_b, allowed) - total)
    weights_b = weights.astype(jnp.bfloat16)
    grad_values = jnp.einsum(
        "kgqp,qkgd->pkd", weights_b, grad_mixed, preferred_element_type=jnp.float32
    )
    grad_weights = jnp.einsum(
        "qkgd,pkd->kgqp", grad_mixed, values_b, preferred_element_type=jnp.float32
    )
    grad_scores = weights * (grad_weights - jnp.sum(weights * grad_weights, axis=-1, keepdims=True))
    grad_scores_b = grad_scores.astype(jnp.bfloat16)
    grouped = queries_b.reshape(rows, kv_count, per, HEAD)
    grad_queries = jnp.einsum(
        "kgqp,pkd->qkgd", grad_scores_b, keys_b, preferred_element_type=jnp.float32
    )
    grad_queries = grad_queries.reshape(rows, q_heads, HEAD) * factor
    grad_keys = (
        jnp.einsum("kgqp,qkgd->pkd", grad_scores_b, grouped, preferred_element_type=jnp.float32)
        * factor
    )
    return (grad_queries, grad_keys, grad_values)


def gate_back(grad_hidden, gate_up, local_ff):
    gate = gate_up[:, :local_ff]
    upper = gate_up[:, local_ff:]
    sigma = jax.nn.sigmoid(gate)
    grad_gate = grad_hidden * upper * sigma * (1.0 + gate * (1.0 - sigma))
    grad_upper = grad_hidden * (gate * sigma)
    return jnp.concatenate([grad_gate, grad_upper], axis=1).astype(jnp.bfloat16)


def attention_forward(field, gain, w_project, w_output, allowed, cosine, sine):
    scale, normed = norm_rows(field, gain)
    project = jnp.dot(normed, w_project, preferred_element_type=jnp.float32)
    queries_b, keys_b, values_b = split_project(project, HEADS, KV_HEADS, cosine, sine)
    mixed, total = attend_forward(queries_b, keys_b, values_b, allowed)
    after = field + jnp.dot(mixed, w_output, preferred_element_type=jnp.float32)
    return (after, (scale, normed, queries_b, keys_b, values_b, total, mixed))


def attention_backward(grad_field, field, gain, w_project, w_output, saved, allowed, cosine, sine):
    scale, normed, queries_b, keys_b, values_b, total, mixed = saved
    grad_branch = grad_field.astype(jnp.bfloat16)
    grad_w_output = contract_rows(mixed, grad_branch)
    grad_mixed = contract_cols(grad_branch, w_output).astype(jnp.bfloat16)
    grad_queries, grad_keys, grad_values = attend_backward(
        grad_mixed, queries_b, keys_b, values_b, total, allowed
    )
    grad_project = join_grads(grad_queries, grad_keys, grad_values, cosine, sine)
    grad_w_project = contract_rows(normed, grad_project)
    grad_normed = contract_cols(grad_project, w_project)
    grad_input, grad_gain = norm_back(grad_normed, field, scale, gain.astype(jnp.float32))
    return (grad_field + grad_input, grad_gain, grad_w_project, grad_w_output)


def mlp_forward(field, gain, w_gateup, w_lower):
    scale, normed = norm_rows(field, gain)
    gate_up = jnp.dot(normed, w_gateup, preferred_element_type=jnp.float32)
    hidden = (jax.nn.silu(gate_up[:, :FF]) * gate_up[:, FF:]).astype(jnp.bfloat16)
    after = field + jnp.dot(hidden, w_lower, preferred_element_type=jnp.float32)
    return (after, (scale, normed, gate_up, hidden))


def mlp_backward(grad_field, field, gain, w_gateup, w_lower, saved):
    scale, normed, gate_up, hidden = saved
    grad_branch = grad_field.astype(jnp.bfloat16)
    grad_w_lower = contract_rows(hidden, grad_branch)
    grad_hidden = contract_cols(grad_branch, w_lower)
    grad_gateup = gate_back(grad_hidden, gate_up, FF)
    grad_w_gateup = contract_rows(normed, grad_gateup)
    grad_normed = contract_cols(grad_gateup, w_gateup)
    grad_input, grad_gain = norm_back(grad_normed, field, scale, gain.astype(jnp.float32))
    return (grad_field + grad_input, grad_gain, grad_w_gateup, grad_w_lower)


def settle(owned):
    return (
        lax.psum(owned[0].astype(jnp.bfloat16), "replica").astype(jnp.float32),
        lax.psum(owned[1].astype(jnp.bfloat16), "replica").astype(jnp.float32),
        lax.psum(owned[2].astype(jnp.bfloat16), "replica").astype(jnp.float32),
        lax.psum(owned[3].astype(jnp.bfloat16), "replica").astype(jnp.float32),
        lax.psum(owned[4].astype(jnp.bfloat16), "replica").astype(jnp.float32),
        lax.psum(owned[5].astype(jnp.bfloat16), "replica").astype(jnp.float32),
    )


def body(
    tokens,
    cotangent,
    seq_lengths,
    seq_device,
    seq_offsets,
    norm_attn,
    w_qkv,
    w_out,
    norm_mlp,
    w_gate_up,
    w_down,
):
    rows = tokens.shape[0]
    layers = w_qkv.shape[0]
    device = lax.axis_index(("shard", "replica"))
    segment, position = locate(device, seq_lengths, seq_device, seq_offsets, rows)
    live = (segment >= 0).astype(jnp.float32)[:, None]
    field = tokens.astype(jnp.float32)
    per_layer = [None] * layers
    cosine, sine = rope_tables(position)
    allowed = mask_of(segment)
    layer = 0
    attn_parts = (
        lax.all_gather(norm_attn[layer], "shard", axis=0, tiled=True),
        lax.all_gather(w_qkv[layer], "shard", axis=0, tiled=True),
        lax.all_gather(w_out[layer], "shard", axis=0, tiled=True),
    )
    middle, attn_saved = attention_forward(
        field, attn_parts[0], attn_parts[1], attn_parts[2], allowed, cosine, sine
    )
    mlp_parts = (
        lax.all_gather(norm_mlp[layer], "shard", axis=0, tiled=True),
        lax.all_gather(w_gate_up[layer], "shard", axis=0, tiled=True),
        lax.all_gather(w_down[layer], "shard", axis=0, tiled=True),
    )
    after, mlp_saved = mlp_forward(middle, mlp_parts[0], mlp_parts[1], mlp_parts[2])
    kept_inputs = [(field, attn_saved, middle, mlp_saved)]
    result = (after * live).astype(jnp.bfloat16)
    grad_field = cotangent.astype(jnp.float32) * live
    for layer in reversed(range(layers)):
        field_in, attn_saved, middle, mlp_saved = kept_inputs[layer]
        mlp_parts = (
            lax.all_gather(norm_mlp[layer], "shard", axis=0, tiled=True),
            lax.all_gather(w_gate_up[layer], "shard", axis=0, tiled=True),
            lax.all_gather(w_down[layer], "shard", axis=0, tiled=True),
        )
        grad_middle, grad_gain_mlp, grad_gateup, grad_lower = mlp_backward(
            grad_field, middle, mlp_parts[0], mlp_parts[1], mlp_parts[2], mlp_saved
        )
        mlp_owned = (
            lax.psum_scatter(
                grad_gain_mlp.astype(jnp.bfloat16), "shard", scatter_dimension=0, tiled=True
            ).astype(jnp.float32),
            lax.psum_scatter(
                grad_gateup.astype(jnp.bfloat16), "shard", scatter_dimension=0, tiled=True
            ).astype(jnp.float32),
            lax.psum_scatter(
                grad_lower.astype(jnp.bfloat16), "shard", scatter_dimension=0, tiled=True
            ).astype(jnp.float32),
        )
        attn_parts = (
            lax.all_gather(norm_attn[layer], "shard", axis=0, tiled=True),
            lax.all_gather(w_qkv[layer], "shard", axis=0, tiled=True),
            lax.all_gather(w_out[layer], "shard", axis=0, tiled=True),
        )
        grad_field, grad_gain_attn, grad_project, grad_output = attention_backward(
            grad_middle,
            field_in,
            attn_parts[0],
            attn_parts[1],
            attn_parts[2],
            attn_saved,
            allowed,
            cosine,
            sine,
        )
        attn_owned = (
            lax.psum_scatter(
                grad_gain_attn.astype(jnp.bfloat16), "shard", scatter_dimension=0, tiled=True
            ).astype(jnp.float32),
            lax.psum_scatter(
                grad_project.astype(jnp.bfloat16), "shard", scatter_dimension=0, tiled=True
            ).astype(jnp.float32),
            lax.psum_scatter(
                grad_output.astype(jnp.bfloat16), "shard", scatter_dimension=0, tiled=True
            ).astype(jnp.float32),
        )
        per_layer[layer] = settle(
            (attn_owned[0], attn_owned[1], attn_owned[2], mlp_owned[0], mlp_owned[1], mlp_owned[2])
        )
    stacked = [jnp.stack([entry[member] for entry in per_layer], axis=0) for member in range(6)]
    return (
        result,
        grad_field,
        stacked[0],
        stacked[1],
        stacked[2],
        stacked[3],
        stacked[4],
        stacked[5],
    )


def solution(mesh):
    placed = (
        P(("shard", "replica"), None),
        P(("shard", "replica"), None),
        P(),
        P(),
        P(),
        P(None, "shard"),
        P(None, "shard", None),
        P(None, "shard", None),
        P(None, "shard"),
        P(None, "shard", None),
        P(None, "shard", None),
    )
    return jax.shard_map(
        body,
        mesh=mesh,
        in_specs=placed,
        out_specs=(
            P(("shard", "replica"), None),
            P(("shard", "replica"), None),
            P(None, "shard"),
            P(None, "shard", None),
            P(None, "shard", None),
            P(None, "shard"),
            P(None, "shard", None),
            P(None, "shard", None),
        ),
        check_vma=False,
    )
```

profile of v0, /device:TPU:0, one launch (start us, length us, event | category | flops | bytes accessed | tf_op | source)
XLA Modules:
  0.0 1345.5 jit_solution(480248952729375393)
XLA Ops:
  10.1 9.6 all-gather
  19.7 8.2 all-gather.3
  28.4 0.7 broadcast_multiply_fusion.1
  30.7 78.1 %all-gather.11.cloned.1.call-done = bf16[1,1536,3072]{2,1,0:T(8,128)(2,1)} async-done(((bf16[1,384,3072]{2,1,0:T(8,128)(2,1)}), bf16[1,1536,3072]{2,1,0:T(8,128)(2,1)}) %all-gather.11.cloned.1.call-update) | async-done | bytes 9437200 | tf_op jit(solution)/shard_map/all_gather | solution.py:244
  108.8 5.2 fusion.10
  114.1 1.3 slice.59
  115.4 0.9 copy.51
  116.6 2.1 copy.53
  118.7 1.1 fusion.57
  120.0 0.8 copy-done.22
  121.2 0.9 fusion.40
  122.1 0.9 exponential_reduce_fusion
  123.1 1.1 copy-done
  124.1 1.1 convolution_convert_fusion.4
  125.3 42.3 %all-gather.13.cloned.1.call-done = bf16[1,1536,1536]{2,1,0:T(8,128)(2,1)} async-done(((bf16[1,384,1536]{2,1,0:T(8,128)(2,1)}), bf16[1,1536,1536]{2,1,0:T(8,128)(2,1)}) %all-gather.13.cloned.1.call-update) | async-done | bytes 4718608 | tf_op jit(solution)/shard_map/all_gather | solution.py:245
  167.6 3.8 multiply_reduce_fusion.2
  171.4 225.6 %all-gather.15.cloned.1.call-done = bf16[1,1536,8192]{2,1,0:T(8,128)(2,1)} async-done(((bf16[1,384,8192]{2,1,0:T(8,128)(2,1)}), bf16[1,1536,8192]{2,1,0:T(8,128)(2,1)}) %all-gather.15.cloned.1.call-update) | async-done | bytes 25165840 | tf_op jit(solution)/shard_map/all_gather | solution.py:252
  397.1 13.8 %fusion.2 = f32[256,8192]{1,0:T(8,128)} fusion(bf16[1,1536,8192]{2,1,0:T(8,128)(2,1)} %all-gather.15.cloned.1.call-done, f32[256,1536]{1,0:T(8,128)S(1)} %get-tuple-element.44, f32[1536]{0:T(1024)S(1)} %convert_reduce_fusion, f32[256]{0:T(256)S(1)} %add_rsqrt_fusion), kind=kOutput, calls=%fused_computation.3 | convolution fusion | flops 6443630592 | bytes 35134464 | tf_op jit(solution)/shard_map/dot_general | solution.py:190
  410.9 110.3 %all-gather.17.cloned.1.call-done = bf16[1,4096,1536]{2,1,0:T(8,128)(2,1)} async-done(((bf16[1,1024,1536]{2,1,0:T(8,128)(2,1)}), bf16[1,4096,1536]{2,1,0:T(8,128)(2,1)}) %all-gather.17.cloned.1.call-update) | async-done | bytes 12582928 | tf_op jit(solution)/shard_map/all_gather | solution.py:253
  521.2 10.4 multiply_convert_fusion.1
  531.6 14.9 %multiply_reduce_fusion = (bf16[1536]{0:T(1024)(128)(2,1)}, f32[256]{0:T(256)S(1)}, f32[256,1536]{1,0:T(8,128)}) fusion(f32[256,1536]{1,0:T(8,128)S(1)} %get-tuple-element.44, f32[256]{0:T(256)S(1)} %add_rsqrt_fusion, f32[1536]{0:T(1024)S(1)} %convert_reduce_fusion, bf16[1,1536,8192]{2,1,0:T(8,128)(2,1)} %all-gather.15.cloned.1.call-done, ...), kind=kOutput, calls=%fused_computation.63 | convolution fusion | flops 6453196800 | bytes 32517120 | tf_op jit(solution)/shard_map/dot_general | solution.py:59
  546.5 2.0 multiply_add_fusion
  548.5 3.6 convolution_convert_fusion.3
  552.2 4.6 fusion.33
  556.8 2.3 copy.56
  559.1 4.2 fusion.16
  563.3 1.2 fusion.18
  565.9 0.8 copy-done.20
  567.0 0.8 broadcast_multiply_fusion
  568.1 0.9 copy-done.12
  569.0 1.1 fusion.53
  570.9 7.3 convolution_convert_fusion.2
  578.3 10.2 convolution_convert_fusion.1
  588.5 14.2 %convolution_convert_fusion = bf16[1536,8192]{1,0:T(8,128)(2,1)} fusion(bf16[256,4096]{1,0:T(8,128)(2,1)} %copy-done.16, bf16[256,4096]{1,0:T(8,128)(2,1)} %copy-done.15, f32[256,1536]{1,0:T(8,128)S(1)} %get-tuple-element.44, f32[1536]{0:T(1024)S(1)} %convert_reduce_fusion, f32[256]{0:T(256)} %copy-done.27), kind=kOutput, calls=%fused_computation | convolution fusion | flops 6464602112 | bytes 30940160 | tf_op jit(solution)/shard_map/dot_general | solution.py:53
  603.0 6.2 reduce-scatter.7.cloned.1.call-done
  609.2 97.9 %reduce-scatter.5.cloned.1.call-done = bf16[384,3072]{1,0:T(8,128)(2,1)} async-done(((bf16[1536,3072]{1,0:T(8,128)(2,1)}), bf16[384,3072]{1,0:T(8,128)(2,1)}) %reduce-scatter.5.cloned.1.call-update) | async-done | bytes 2359312 | tf_op jit(solution)/shard_map/reduce_scatter | solution.py:300
  707.1 124.3 %reduce-scatter.11.cloned.1.call-done = bf16[1024,1536]{1,0:T(8,128)(2,1)} async-done(((bf16[4096,1536]{1,0:T(8,128)(2,1)}), bf16[1024,1536]{1,0:T(8,128)(2,1)}) %reduce-scatter.11.cloned.1.call-update) | async-done | bytes 3145744 | tf_op jit(solution)/shard_map/reduce_scatter | solution.py:276
  831.4 224.9 %reduce-scatter.9.cloned.1.call-done = bf16[384,8192]{1,0:T(8,128)(2,1)} async-done(((bf16[1536,8192]{1,0:T(8,128)(2,1)}), bf16[384,8192]{1,0:T(8,128)(2,1)}) %reduce-scatter.9.cloned.1.call-update) | async-done | bytes 6291472 | tf_op jit(solution)/shard_map/reduce_scatter | solution.py:273
  1058.2 8.8 fusion.46
  1067.0 9.2 all-reduce.4
  1076.4 15.4 %all-reduce.2 = (bf16[1,384]{1,0:T(2,128)(2,1)S(1)}, bf16[1,384]{1,0:T(2,128)(2,1)S(1)}) all-reduce(bf16[1,384]{1,0:T(2,128)(2,1)S(1)} %stack.36, bf16[1,384]{1,0:T(2,128)(2,1)S(1)} %stack.42), channel_id=1, replica_groups=mesh['shard'=4,'replica'=8] {'replica'}, use_global_device_ids=true, to_apply=%region_11.12 | all-reduce | flops 768 | bytes 3072 | tf_op jit(solution)/shard_map/psum | solution.py:210
  1093.6 3.4 fusion.45
  1096.9 9.0 fusion.30
  1105.9 215.4 %all-reduce.7.cloned.1.call-done = (bf16[1,384,3072]{2,1,0:T(8,128)(2,1)}, bf16[1,384,1536]{2,1,0:T(8,128)(2,1)}, bf16[1,384,8192]{2,1,0:T(8,128)(2,1)}, bf16[1,1024,1536]{2,1,0:T(8,128)(2,1)}) async-done(((bf16[1,384,3072]{2,1,0:T(8,128)(2,1)}, bf16[1,384,1536]{2,1,0:T(8,128)(2,1)}, bf16[1,384,8192]{2,1,0:T(8,128)(2,1)}, bf16[1,1024,1536]{2,1,0:T(8,128)(2,1)}), (bf16[1,384,3072]{2,1,0:T(8,128)(2,1)}, ...) | async-done | bytes 12976144 | tf_op jit(solution)/shard_map/psum | solution.py:211
  1321.3 4.6 stack.39
  1325.9 3.0 stack.41
  1328.8 6.3 stack.45
  1335.2 3.6 stack.47
  (132 shorter events, 12.1 us)
Async XLA Ops:
  7.2 101.6 %all-gather.11.cloned.1.call-start = ((), (), s32[]{:S(2)}) async-start(), calls=%async_computation.8 | async-start | bytes 11796480 | tf_op jit(solution)/shard_map/all_gather | solution.py:244
  7.9 159.7 %all-gather.13.cloned.1.call-start = ((), (), s32[]{:S(2)}) async-start(), calls=%async_computation.9 | async-start | bytes 5898240 | tf_op jit(solution)/shard_map/all_gather | solution.py:245
  8.7 388.4 %all-gather.15.cloned.1.call-start = ((), (), s32[]{:S(2)}) async-start(), calls=%async_computation.10 | async-start | bytes 31457280 | tf_op jit(solution)/shard_map/all_gather | solution.py:252
  9.4 10.3 copy-start.36
  9.4 18.5 %copy-start.39 = (s32[64]{0:T(128)S(1)}, s32[64]{0:T(128)}, u32[]{:S(2)}) copy-start(s32[64]{0:T(128)} %param.14) | copy-start | bytes 772
  9.4 18.6 %copy-start.37 = (s32[64]{0:T(128)S(1)}, s32[64]{0:T(128)}, u32[]{:S(2)}) copy-start(s32[64]{0:T(128)} %param.15) | copy-start | bytes 772
  9.4 18.6 %copy-start.38 = (s32[64]{0:T(128)S(1)}, s32[64]{0:T(128)}, u32[]{:S(2)}) copy-start(s32[64]{0:T(128)} %param.13) | copy-start | bytes 772
  9.4 19.7 %copy-start.2 = (bf16[256,1536]{1,0:T(8,128)(2,1)S(1)}, bf16[256,1536]{1,0:T(8,128)(2,1)}, u32[]{:S(2)}) copy-start(bf16[256,1536]{1,0:T(8,128)(2,1)} %param.11) | copy-start | bytes 2359300
  9.4 511.8 %all-gather.17.cloned.1.call-start = ((), (), s32[]{:S(2)}) async-start(), calls=%async_computation.11 | async-start | bytes 15728640 | tf_op jit(solution)/shard_map/all_gather | solution.py:253
  10.0 599.2 %reduce-scatter.7.cloned.1.call-start = ((), (), s32[]{:S(2)}) async-start(), calls=%async_computation.5 | async-start | bytes 5898240 | tf_op jit(solution)/shard_map/reduce_scatter | solution.py:303
  29.4 84.6 %copy-start.28 = (f32[256]{0:T(256)}, f32[256]{0:T(256)S(1)}, u32[]{:S(2)}) copy-start(f32[256]{0:T(256)S(1)} %add_rsqrt_fusion.1) | copy-start | bytes 3076
  119.9 0.9 copy-start.22
  119.9 1.0 copy-start.23
  120.0 1.2 copy-start.17
  121.2 0.9 copy-start.6
  122.1 2.0 copy-start
  122.1 2.0 copy-start.19
  123.1 2.2 copy-start.25
  125.3 46.1 %copy-start.4 = (bf16[8,96,2,256]{3,1,2,0:T(8,128)(2,1)}, bf16[8,96,2,256]{3,1,2,0:T(8,128)(2,1)S(1)}, u32[]{:S(2)}) copy-start(bf16[8,96,2,256]{3,1,2,0:T(8,128)(2,1)S(1)} %convolution_convert_fusion.4) | copy-start | bytes 2359300
  171.4 360.2 %copy-start.27 = (f32[256]{0:T(256)}, f32[256]{0:T(256)S(1)}, u32[]{:S(2)}) copy-start(f32[256]{0:T(256)S(1)} %add_rsqrt_fusion) | copy-start | bytes 3076
  397.1 124.1 %copy-start.10 = (bf16[256,1536]{1,0:T(8,128)(2,1)S(1)}, bf16[256,1536]{1,0:T(8,128)(2,1)}, u32[]{:S(2)}) copy-start(bf16[256,1536]{1,0:T(8,128)(2,1)} %param.12) | copy-start | bytes 2359300
  397.1 124.1 %copy-start.31 = (f32[256]{0:T(256)S(1)}, f32[256]{0:T(256)}, u32[]{:S(2)}) copy-start(f32[256]{0:T(256)} %compare_convert_fusion) | copy-start | bytes 3076
  531.6 14.9 %copy-start.15 = (bf16[256,4096]{1,0:T(8,128)(2,1)}, bf16[256,4096]{1,0:T(8,128)(2,1)S(1)}, u32[]{:S(2)}) copy-start(bf16[256,4096]{1,0:T(8,128)(2,1)S(1)} %get-tuple-element.22) | copy-start | bytes 6291460
  531.6 14.9 %copy-start.16 = (bf16[256,4096]{1,0:T(8,128)(2,1)}, bf16[256,4096]{1,0:T(8,128)(2,1)S(1)}, u32[]{:S(2)}) copy-start(bf16[256,4096]{1,0:T(8,128)(2,1)S(1)} %get-tuple-element.23) | copy-start | bytes 6291460
  531.6 14.9 %copy-start.11 = (bf16[256,1536]{1,0:T(8,128)(2,1)S(1)}, bf16[256,1536]{1,0:T(8,128)(2,1)}, u32[]{:S(2)}) copy-start(bf16[256,1536]{1,0:T(8,128)(2,1)} %param.12) | copy-start | bytes 2359300
  531.6 14.9 %copy-start.32 = (f32[256]{0:T(256)S(1)}, f32[256]{0:T(256)}, u32[]{:S(2)}) copy-start(f32[256]{0:T(256)} %compare_convert_fusion) | copy-start | bytes 3076
  546.5 2.0 copy-start.5
  552.1 155.0 %reduce-scatter.5.cloned.1.call-start = ((), (), s32[]{:S(2)}) async-start(), calls=%async_computation.4 | async-start | bytes 11796480 | tf_op jit(solution)/shard_map/reduce_scatter | solution.py:300
  559.1 4.2 copy-start.1
  559.1 4.2 copy-start.18
  559.1 4.2 copy-start.26
  564.6 0.9 copy-start.21
  565.7 0.9 copy-start.20
  565.9 1.2 copy-start.7
  567.0 3.1 copy-start.14
  567.8 1.1 copy-start.12
  568.9 1.9 copy-start.3
  569.0 1.9 copy-start.29
  570.1 0.7 copy-start.24
  578.2 253.2 %reduce-scatter.11.cloned.1.call-start = ((), (), s32[]{:S(2)}) async-start(), calls=%async_computation.7 | async-start | bytes 15728640 | tf_op jit(solution)/shard_map/reduce_scatter | solution.py:276
  588.5 467.8 %reduce-scatter.9.cloned.1.call-start = ((), (), s32[]{:S(2)}) async-start(), calls=%async_computation.6 | async-start | bytes 31457280 | tf_op jit(solution)/shard_map/reduce_scatter | solution.py:273
  602.8 718.6 %all-reduce.7.cloned.1.call-start = ((), (), s32[]{:S(2)}) async-start(), calls=%async_computation.12 | async-start | bytes 25952256 | tf_op jit(solution)/shard_map/psum | solution.py:211
  1056.3 1.9 copy-start.30
  1058.2 8.8 copy-start.34
  1093.6 3.4 copy-start.9
  1093.6 3.4 copy-start.33
  1321.3 7.5 copy-start.8
  1328.8 6.3 copy-start.13
  (2 other events, 1.3 us)
Sparse Core Ops, SparseCore 0:
  9.8 98.9 all-gather.10
  110.6 56.9 all-gather.12
  169.5 227.5 all-gather.14
  398.8 122.4 all-gather.16
  552.3 56.9 reduce-scatter.6
  612.2 94.8 reduce-scatter.4
  710.8 120.5 reduce-scatter.10
  834.5 221.7 reduce-scatter.8
  1058.9 262.3 all-reduce.6
where the time goes:
time: 1350 us
  waiting for transfers between devices  1130 us (84%)
  matrix products  114 us (8%)
  blocking collectives  42.4 us (3%)
  other arithmetic  32 us (2%)
  between operations  15.3 us (1%)
    all_gather x1, waiting for transfers between devices, body(): lax.all_gather(w_gate_up[layer], 'shard', axis=0, tiled=True)  226 us
    reduce_scatter x1, waiting for transfers between devices, body(): lax.psum_scatter(grad_gateup.astype(jnp.bfloat16), 'shard', scatter_dimen...  225 us
    psum x1, waiting for transfers between devices, settle(): lax.psum(owned[1].astype(jnp.bfloat16), 'replica').astype(jnp.float32)  215 us
    reduce_scatter x1, waiting for transfers between devices, body(): lax.psum_scatter(grad_lower.astype(jnp.bfloat16), 'shard', scatter_dimens...  124 us
    all_gather x1, waiting for transfers between devices, body(): lax.all_gather(w_down[layer], 'shard', axis=0, tiled=True)  110 us
    reduce_scatter x1, waiting for transfers between devices, body(): lax.psum_scatter(grad_project.astype(jnp.bfloat16), 'shard', scatter_dime...  97.9 us
    all_gather x1, waiting for transfers between devices, body(): lax.all_gather(w_qkv[layer], 'shard', axis=0, tiled=True)  78.1 us
    all_gather x1, waiting for transfers between devices, body(): lax.all_gather(w_out[layer], 'shard', axis=0, tiled=True)  42.3 us
  transfers between devices with their start and end apart: 9, of which 9 were waited for; matrix products, arithmetic and copies ran while one was open for 8% of the time, Pallas kernels for 0%

commit v1 on v0

--- a/solution.py
+++ b/solution.py
@@ -208,7 +208,9 @@
 def settle(owned):
     return (
         lax.psum(owned[0].astype(jnp.bfloat16), "replica").astype(jnp.float32),
-        lax.psum(owned[1].astype(jnp.bfloat16), "replica").astype(jnp.float32),
+        jnp.sum(lax.all_gather(owned[1].astype(jnp.bfloat16), "replica"), axis=0).astype(
+            jnp.float32
+        ),
         lax.psum(owned[2].astype(jnp.bfloat16), "replica").astype(jnp.float32),
         lax.psum(owned[3].astype(jnp.bfloat16), "replica").astype(jnp.float32),
         lax.psum(owned[4].astype(jnp.bfloat16), "replica").astype(jnp.float32),

time: 1350 us -> 1500 us (1.11)
  waiting for transfers between devices: 1130 us -> 1250 us
  other arithmetic: 32 us -> 47.5 us
    all_gather x0 -> x1, waiting for transfers between devices: none -> 119 us  [settle(): lax.all_gather(owned[1].astype(jnp.bfloat16), 'replica')]
    reduce_scatter x1, waiting for transfers between devices: 6.24 us -> 60.3 us  [body(): lax.psum_scatter(grad_output.astype(jnp.bfloat16), 'shard', scatter_dimen...]
    reduce_scatter x1, waiting for transfers between devices: 97.9 us -> 64.5 us  [body(): lax.psum_scatter(grad_project.astype(jnp.bfloat16), 'shard', scatter_dime...]
  transfers between devices with their start and end apart: 9 -> 10, of which waited for: 9 -> 10; matrix products, arithmetic and copies ran while one was open for 8% -> 7% of each run, Pallas kernels for 0% -> 0%
where the time goes in v1:
time: 1500 us; the launch traced here: 1490 us
  waiting for transfers between devices  1250 us (83%)
  matrix products  114 us (8%)
  other arithmetic  47.5 us (3%)
  blocking collectives  43.5 us (3%)
  between operations  15.8 us (1%)
    all_gather x1, waiting for transfers between devices, body(): lax.all_gather(w_gate_up[layer], 'shard', axis=0, tiled=True)  226 us
    reduce_scatter x1, waiting for transfers between devices, body(): lax.psum_scatter(grad_gateup.astype(jnp.bfloat16), 'shard', scatter_dimen...  225 us
    psum x1, waiting for transfers between devices, settle(): lax.psum(owned[2].astype(jnp.bfloat16), 'replica').astype(jnp.float32)  201 us
    reduce_scatter x1, waiting for transfers between devices, body(): lax.psum_scatter(grad_lower.astype(jnp.bfloat16), 'shard', scatter_dimens...  124 us
    all_gather x1, waiting for transfers between devices, settle(): lax.all_gather(owned[1].astype(jnp.bfloat16), 'replica')  119 us
    all_gather x1, waiting for transfers between devices, body(): lax.all_gather(w_down[layer], 'shard', axis=0, tiled=True)  110 us
    all_gather x1, waiting for transfers between devices, body(): lax.all_gather(w_qkv[layer], 'shard', axis=0, tiled=True)  78 us
    reduce_scatter x1, waiting for transfers between devices, body(): lax.psum_scatter(grad_project.astype(jnp.bfloat16), 'shard', scatter_dime...  64.5 us
  transfers between devices with their start and end apart: 10, of which 10 were waited for; matrix products, arithmetic and copies ran while one was open for 7% of the time, Pallas kernels for 0%

profile of v1, /device:TPU:0, one launch (start us, length us, event | category | flops | bytes accessed | tf_op | source)
XLA Modules:
  0.0 1488.2 jit_solution(4158816531419952068)
XLA Ops:
  10.1 9.6 all-gather
  19.7 8.2 all-gather.3
  28.4 0.8 broadcast_multiply_fusion.1
  30.7 78.0 %all-gather.13.cloned.1.call-done = bf16[1,1536,3072]{2,1,0:T(8,128)(2,1)} async-done(((bf16[1,384,3072]{2,1,0:T(8,128)(2,1)}), bf16[1,1536,3072]{2,1,0:T(8,128)(2,1)}) %all-gather.13.cloned.1.call-update) | async-done | bytes 9437200 | tf_op jit(solution)/shard_map/all_gather | solution.py:246
  108.8 5.2 fusion.10
  114.2 1.3 slice.59
  115.5 0.9 copy.51
  116.6 2.1 copy.53
  118.8 1.1 fusion.57
  120.1 0.8 copy-done.19
  121.3 0.9 fusion.40
  122.2 0.9 exponential_reduce_fusion
  123.1 1.1 copy-done
  124.2 1.1 convolution_convert_fusion.4
  125.3 42.3 %all-gather.15.cloned.1.call-done = bf16[1,1536,1536]{2,1,0:T(8,128)(2,1)} async-done(((bf16[1,384,1536]{2,1,0:T(8,128)(2,1)}), bf16[1,1536,1536]{2,1,0:T(8,128)(2,1)}) %all-gather.15.cloned.1.call-update) | async-done | bytes 4718608 | tf_op jit(solution)/shard_map/all_gather | solution.py:247
  167.6 3.8 multiply_reduce_fusion.2
  171.4 225.6 %all-gather.17.cloned.1.call-done = bf16[1,1536,8192]{2,1,0:T(8,128)(2,1)} async-done(((bf16[1,384,8192]{2,1,0:T(8,128)(2,1)}), bf16[1,1536,8192]{2,1,0:T(8,128)(2,1)}) %all-gather.17.cloned.1.call-update) | async-done | bytes 25165840 | tf_op jit(solution)/shard_map/all_gather | solution.py:254
  397.1 13.8 fusion.2
  410.9 110.3 %all-gather.19.cloned.1.call-done = bf16[1,4096,1536]{2,1,0:T(8,128)(2,1)} async-done(((bf16[1,1024,1536]{2,1,0:T(8,128)(2,1)}), bf16[1,4096,1536]{2,1,0:T(8,128)(2,1)}) %all-gather.19.cloned.1.call-update) | async-done | bytes 12582928 | tf_op jit(solution)/shard_map/all_gather | solution.py:255
  521.2 11.2 multiply_convert_fusion.1
  532.4 14.8 multiply_reduce_fusion
  547.2 1.9 multiply_add_fusion
  549.2 2.3 fusion.33
  551.5 2.3 copy.56
  553.8 3.6 fusion.53
  557.9 1.4 fusion.16
  559.3 1.2 fusion.18
  562.9 0.8 copy-done.17
  564.9 7.1 convolution_convert_fusion.2
  572.3 4.7 convolution_convert_fusion.3
  577.1 10.4 convolution_convert_fusion.1
  587.5 15.0 %convolution_convert_fusion = bf16[1536,8192]{1,0:T(8,128)(2,1)} fusion(bf16[256,4096]{1,0:T(8,128)(2,1)} %get-tuple-element.22, bf16[256,4096]{1,0:T(8,128)(2,1)} %get-tuple-element.21, f32[256,1536]{1,0:T(8,128)S(1)} %get-tuple-element.43, f32[1536]{0:T(1024)S(1)} %convert_reduce_fusion, f32[256]{0:T(256)} %copy-done.24), kind=kOutput, calls=%fused_computation | convolution fusion | flops 6464602112 | bytes 30940160 | tf_op jit(solution)/shard_map/dot_general | solution.py:53
  602.6 64.5 %reduce-scatter.5.cloned.1.call-done = bf16[384,3072]{1,0:T(8,128)(2,1)} async-done(((bf16[1536,3072]{1,0:T(8,128)(2,1)}), bf16[384,3072]{1,0:T(8,128)(2,1)}) %reduce-scatter.5.cloned.1.call-update) | async-done | bytes 2359312 | tf_op jit(solution)/shard_map/reduce_scatter | solution.py:302
  667.2 60.3 %reduce-scatter.7.cloned.1.call-done = bf16[384,1536]{1,0:T(8,128)(2,1)} async-done(((bf16[1536,1536]{1,0:T(8,128)(2,1)}), bf16[384,1536]{1,0:T(8,128)(2,1)}) %reduce-scatter.7.cloned.1.call-update) | async-done | bytes 1179664 | tf_op jit(solution)/shard_map/reduce_scatter | solution.py:305
  727.5 124.3 %reduce-scatter.11.cloned.1.call-done = bf16[1024,1536]{1,0:T(8,128)(2,1)} async-done(((bf16[4096,1536]{1,0:T(8,128)(2,1)}), bf16[1024,1536]{1,0:T(8,128)(2,1)}) %reduce-scatter.11.cloned.1.call-update) | async-done | bytes 3145744 | tf_op jit(solution)/shard_map/reduce_scatter | solution.py:278
  851.8 224.8 %reduce-scatter.9.cloned.1.call-done = bf16[384,8192]{1,0:T(8,128)(2,1)} async-done(((bf16[1536,8192]{1,0:T(8,128)(2,1)}), bf16[384,8192]{1,0:T(8,128)(2,1)}) %reduce-scatter.9.cloned.1.call-update) | async-done | bytes 6291472 | tf_op jit(solution)/shard_map/reduce_scatter | solution.py:275
  1078.6 8.8 fusion.46
  1087.3 9.2 all-reduce.4
  1096.7 16.5 %all-reduce.2 = (bf16[1,384]{1,0:T(2,128)(2,1)S(1)}, bf16[1,384]{1,0:T(2,128)(2,1)S(1)}) all-reduce(bf16[1,384]{1,0:T(2,128)(2,1)S(1)} %stack.31, bf16[1,384]{1,0:T(2,128)(2,1)S(1)} %stack.35), channel_id=1, replica_groups=mesh['shard'=4,'replica'=8] {'replica'}, use_global_device_ids=true, to_apply=%region_11.12 | all-reduce | flops 768 | bytes 3072 | tf_op jit(solution)/shard_map/psum | solution.py:210
  1115.0 3.4 fusion.45
  1118.4 9.1 fusion.30
  1127.4 119.5 %all-gather.21.cloned.1.call-done = bf16[3072,3072]{1,0:T(8,128)(2,1)} async-done(((bf16[384,3072]{1,0:T(8,128)(2,1)}), bf16[3072,3072]{1,0:T(8,128)(2,1)}) %all-gather.21.cloned.1.call-update) | async-done | bytes 18874384 | tf_op jit(solution)/shard_map/all_gather | solution.py:211
  1246.9 12.6 reduce_sum.101
  1259.5 4.5 bitcast_convert_fusion
  1264.0 201.1 %all-reduce.7.cloned.1.call-done = (bf16[1,384,1536]{2,1,0:T(8,128)(2,1)}, bf16[1,384,8192]{2,1,0:T(8,128)(2,1)}, bf16[1,1024,1536]{2,1,0:T(8,128)(2,1)}) async-done(((bf16[1,384,1536]{2,1,0:T(8,128)(2,1)}, bf16[1,384,8192]{2,1,0:T(8,128)(2,1)}, bf16[1,1024,1536]{2,1,0:T(8,128)(2,1)}), (bf16[1,384,1536]{2,1,0:T(8,128)(2,1)}, bf16[1,384,8192]{2,1,0:T(8,128)(2,1)}, ...) | async-done | bytes 10616848 | tf_op jit(solution)/shard_map/psum | solution.py:214
  1465.1 3.0 stack.34
  1468.1 9.3 stack.38
  1477.4 3.6 stack.40
  (135 shorter events, 13.5 us)
Async XLA Ops:
  7.2 101.6 %all-gather.13.cloned.1.call-start = ((), (), s32[]{:S(2)}) async-start(), calls=%async_computation.8 | async-start | bytes 11796480 | tf_op jit(solution)/shard_map/all_gather | solution.py:246
  7.9 159.7 %all-gather.15.cloned.1.call-start = ((), (), s32[]{:S(2)}) async-start(), calls=%async_computation.9 | async-start | bytes 5898240 | tf_op jit(solution)/shard_map/all_gather | solution.py:247
  8.7 388.4 %all-gather.17.cloned.1.call-start = ((), (), s32[]{:S(2)}) async-start(), calls=%async_computation.10 | async-start | bytes 31457280 | tf_op jit(solution)/shard_map/all_gather | solution.py:254
  9.4 10.3 copy-start.33
  9.4 18.5 %copy-start.36 = (s32[64]{0:T(128)S(1)}, s32[64]{0:T(128)}, u32[]{:S(2)}) copy-start(s32[64]{0:T(128)} %param.14) | copy-start | bytes 772
  9.4 18.6 %copy-start.34 = (s32[64]{0:T(128)S(1)}, s32[64]{0:T(128)}, u32[]{:S(2)}) copy-start(s32[64]{0:T(128)} %param.15) | copy-start | bytes 772
  9.4 18.6 %copy-start.35 = (s32[64]{0:T(128)S(1)}, s32[64]{0:T(128)}, u32[]{:S(2)}) copy-start(s32[64]{0:T(128)} %param.13) | copy-start | bytes 772
  9.4 19.7 %copy-start.2 = (bf16[256,1536]{1,0:T(8,128)(2,1)S(1)}, bf16[256,1536]{1,0:T(8,128)(2,1)}, u32[]{:S(2)}) copy-start(bf16[256,1536]{1,0:T(8,128)(2,1)} %param.11) | copy-start | bytes 2359300
  9.4 511.8 %all-gather.19.cloned.1.call-start = ((), (), s32[]{:S(2)}) async-start(), calls=%async_computation.11 | async-start | bytes 15728640 | tf_op jit(solution)/shard_map/all_gather | solution.py:255
  10.0 657.1 %reduce-scatter.5.cloned.1.call-start = ((), (), s32[]{:S(2)}) async-start(), calls=%async_computation.4 | async-start | bytes 11796480 | tf_op jit(solution)/shard_map/reduce_scatter | solution.py:302
  29.4 84.6 %copy-start.25 = (f32[256]{0:T(256)}, f32[256]{0:T(256)S(1)}, u32[]{:S(2)}) copy-start(f32[256]{0:T(256)S(1)} %add_rsqrt_fusion.1) | copy-start | bytes 3076
  119.9 0.9 copy-start.19
  119.9 1.0 copy-start.20
  120.0 1.2 copy-start.13
  121.2 0.9 copy-start.5
  122.1 2.0 copy-start
  122.1 2.0 copy-start.15
  123.1 2.2 copy-start.22
  125.3 46.1 %copy-start.4 = (bf16[8,96,2,256]{3,1,2,0:T(8,128)(2,1)}, bf16[8,96,2,256]{3,1,2,0:T(8,128)(2,1)S(1)}, u32[]{:S(2)}) copy-start(bf16[8,96,2,256]{3,1,2,0:T(8,128)(2,1)S(1)} %convolution_convert_fusion.4) | copy-start | bytes 2359300
  171.4 361.0 %copy-start.24 = (f32[256]{0:T(256)}, f32[256]{0:T(256)S(1)}, u32[]{:S(2)}) copy-start(f32[256]{0:T(256)S(1)} %add_rsqrt_fusion) | copy-start | bytes 3076
  397.1 124.2 %copy-start.8 = (bf16[256,1536]{1,0:T(8,128)(2,1)S(1)}, bf16[256,1536]{1,0:T(8,128)(2,1)}, u32[]{:S(2)}) copy-start(bf16[256,1536]{1,0:T(8,128)(2,1)} %param.12) | copy-start | bytes 2359300
  397.1 124.2 %copy-start.28 = (f32[256]{0:T(256)S(1)}, f32[256]{0:T(256)}, u32[]{:S(2)}) copy-start(f32[256]{0:T(256)} %compare_convert_fusion) | copy-start | bytes 3076
  521.2 27.9 %slice-start = ((s8[4718592]{0:T(1024)(128)(4,1)}), s8[4194304]{0:T(1024)(128)(4,1)S(1)}, s32[]{:S(2)}) async-start(s8[4718592]{0:T(1024)(128)(4,1)} %bitcast.134), calls=%async_computation.14 | async-start | bytes 8388608
  532.4 14.8 copy-start.9
  532.4 14.8 copy-start.29
  532.4 16.7 %slice-start.1 = ((s8[4718592]{0:T(1024)(128)(4,1)}), s8[524288]{0:T(1024)(128)(4,1)S(1)}, s32[]{:S(2)}) async-start(s8[4718592]{0:T(1024)(128)(4,1)} %bitcast.134), calls=%async_computation.15 | async-start | bytes 1048576
  553.8 3.7 copy-start.1
  553.8 3.9 copy-start.10
  553.8 3.9 copy-start.14
  553.8 4.0 copy-start.16
  553.8 4.0 copy-start.23
  557.8 6.3 copy-start.21
  560.5 1.1 copy-start.6
  560.5 1.1 copy-start.18
  562.8 0.9 copy-start.17
  563.7 1.2 copy-start.3
  563.7 1.2 copy-start.26
  564.0 0.9 copy-start.12
  572.0 155.5 %reduce-scatter.7.cloned.1.call-start = ((), (), s32[]{:S(2)}) async-start(), calls=%async_computation.5 | async-start | bytes 5898240 | tf_op jit(solution)/shard_map/reduce_scatter | solution.py:305
  577.0 274.8 %reduce-scatter.11.cloned.1.call-start = ((), (), s32[]{:S(2)}) async-start(), calls=%async_computation.7 | async-start | bytes 15728640 | tf_op jit(solution)/shard_map/reduce_scatter | solution.py:278
  587.5 489.2 %reduce-scatter.9.cloned.1.call-start = ((), (), s32[]{:S(2)}) async-start(), calls=%async_computation.6 | async-start | bytes 31457280 | tf_op jit(solution)/shard_map/reduce_scatter | solution.py:275
  602.6 644.4 %all-gather.21.cloned.1.call-start = ((), (), s32[]{:S(2)}) async-start(), calls=%async_computation.12 | async-start | bytes 21233664 | tf_op jit(solution)/shard_map/all_gather | solution.py:211
  667.1 798.0 %all-reduce.7.cloned.1.call-start = ((), (), s32[]{:S(2)}) async-start(), calls=%async_computation.13 | async-start | bytes 21233664 | tf_op jit(solution)/shard_map/psum | solution.py:214
  1076.7 1.9 copy-start.27
  1078.6 8.8 copy-start.31
  1115.0 3.4 copy-start.7
  1115.0 3.4 copy-start.30
  1468.1 9.3 copy-start.11
  (2 other events, 1.3 us)
Sparse Core Ops, SparseCore 0:
  9.8 98.9 all-gather.12
  110.6 56.9 all-gather.14
  169.5 227.5 all-gather.16
  398.8 122.4 all-gather.18
  572.1 94.8 reduce-scatter.4
  670.5 56.9 reduce-scatter.6
  731.2 120.6 reduce-scatter.10
  854.9 221.6 reduce-scatter.8
  1078.3 168.5 all-gather.20
  1249.4 215.7 all-reduce.6
